TPU v7x, 128 devices: a whole 4x4x4 slice. The times are simulated.
128 devices in a mesh: row: 8 (over x, core), col: 16 (over z, y).
Axes of the slice: x: 4, y: 4, z: 4, core: 2. Of those that a mesh axis runs over, the one named last changes fastest.
Arguments:
- tail_vectors: float32 [64512, 4096], P('row', 'col'), may hold values from -6 to 6
- lower_panel: float32 [64512, 1024], P(('row', 'col')), may hold values from -0.0234375 to 0.0234375
- window_rhs: float32 [1024, 4096], P('row', 'col'), may hold values from -6 to 6
- window_block: float32 [1024, 1024], P(('row', 'col')), may hold values from -1 to 2, as said below
Outputs:
- window_vectors: float32 [1024, 4096], P('row', 'col')
Inputs may be any that keep to these rules, and one draw needn't show every extreme that they name: window_block is zero above the diagonal; its diagonal lies in 1 to 2; entries below the diagonal are under 1 / sqrt(1024) in magnitude.
All inputs are finite; a program needn't handle non-finite values.
Results may differ from a plain program's by a relative error of at most 0.000082.
Values sent between devices are 32-bit elements; how exact they have to be, the bound alone decides.
A program may use at most 128 MiB of HBM per device.

v0:
```python
import functools

import jax
import jax.numpy as jnp
from jax import lax
from jax.experimental import pallas as pl
from jax.experimental.pallas import tpu as pltpu
from jax.sharding import PartitionSpec as P

MESH = pl.DeviceIdType.MESH
HIGHEST = lax.Precision.HIGHEST
F32 = jnp.float32
BF16 = jnp.bfloat16
SIDE = 4
PLACE = (0, 1, 3, 2)
PARTS = 3


def dot(a, b):
    return jnp.dot(a, b, precision=HIGHEST, preferred_element_type=F32)


def dot_t(a, b):
    return lax.dot_general(a, b, (((0,), (0,)), ((), ())), precision=HIGHEST, preferred_element_type=F32)


def mm(a, b):
    return jnp.dot(a, b, preferred_element_type=F32)


def halves(a):
    high = a.astype(BF16)
    return high, (a - high.astype(F32)).astype(BF16)


def lower_inverse(block, base=32):
    size = block.shape[0]
    rows = lax.broadcasted_iota(jnp.int32, (size, size), 0)
    cols = lax.broadcasted_iota(jnp.int32, (size, size), 1)
    eye = jnp.where(rows == cols, 1.0, 0.0)
    diag_col = jnp.sum(jnp.where(rows == cols, block, 0.0), axis=1, keepdims=True)
    diag_row = jnp.sum(jnp.where(rows == cols, block, 0.0), axis=0, keepdims=True)
    near = (rows // base == cols // base) & (rows > cols)
    power = jnp.where(near, -block / diag_col, 0.0)
    inverse = eye + power
    reach = 2
    while reach < base:
        power = dot(power, power)
        inverse = inverse + dot(inverse, power)
        reach *= 2
    inverse = inverse / diag_row
    while base < size:
        below = (rows // (2 * base) == cols // (2 * base)) & (rows // base > cols // base)
        inverse = inverse - dot(dot(inverse, jnp.where(below, block, 0.0)), inverse)
        base *= 2
    return inverse


def kernel(
    tail_hbm, panel_hbm, block_hbm, rhs_hbm, out_ref,
    tbuf, relay, pbuf, phi, plo, pthi, ptlo, wall, inv, inv_hi, inv_lo, tmp, rhs, thi, tlo,
    sums, core_in, first_in, second_in, last_in,
    local_sem, wz_s, wz_r, wy_s, wy_r, wa_s, wa_r, wb_s, wb_r, wc_s, wc_r,
    p_s, p_r, t_s, t_r, r_s, r_r, f_s, f_r,
    c_s, c_r, a_s, a_r, b_s, b_r, l_s, l_r,
):
    depth, window = panel_hbm.shape
    thin = block_hbm.shape[0]
    share, width = rhs_hbm.shape
    lane = width // 2
    pad = pbuf.shape[1]
    part = depth // PARTS
    r = lax.axis_index("row")
    c = lax.axis_index("col")
    x, k = r // 2, r % 2
    z, y = c // SIDE, c % SIDE
    step = 1 - 2 * k
    low, mirror = x + 1 - 2 * (x % 2), SIDE - 1 - x
    p1 = k * mirror + (1 - k) * low
    p2 = k * low + (1 - k) * mirror
    p12 = (x + 2) % SIDE

    def at_z(d):
        return {"col": ((z + d + SIDE) % SIDE) * SIDE + y}

    def at_y(d):
        return {"col": z * SIDE + (y + d + SIDE) % SIDE}

    def at_x(other):
        return {"row": 2 * other + k}

    partner = {"row": 2 * x + 1 - k}
    pending = []

    def remote(src, dst, send, recv, where):
        return pltpu.make_async_remote_copy(
            src_ref=src, dst_ref=dst, send_sem=send, recv_sem=recv, device_id=where, device_id_type=MESH
        )

    def go(src, dst, send, recv, where, keep=True):
        copy = remote(src, dst, send, recv, where)
        copy.start()
        if keep:
            pending.append(copy)
        return copy

    def arrived(dst, send, recv):
        remote(dst, dst, send, recv, partner).wait_recv()

    def owner_rows(dz, dy):
        owner = ((z + dz + SIDE) % SIDE) * SIDE + (y + dy) % SIDE
        return pl.ds(pl.multiple_of(owner * depth, 8), depth)

    def rows_of(index, size=128):
        return pl.ds(pl.multiple_of(index * size, size), size)

    own_thin = wall.at[r, pl.ds(pl.multiple_of(c * thin, 8), thin)]
    locals_ = [
        pltpu.make_async_copy(block_hbm, own_thin, local_sem.at[0]),
        pltpu.make_async_copy(panel_hbm, pbuf.at[0, pl.ds(0, depth)], local_sem.at[1]),
        pltpu.make_async_copy(rhs_hbm, rhs, local_sem.at[2]),
    ] + [
        pltpu.make_async_copy(tail_hbm.at[owner_rows(0, d)], tbuf.at[0, PLACE[d], pl.ds(0, depth)], local_sem.at[3 + d])
        for d in range(SIDE)
    ]
    for copy in locals_:
        copy.start()

    barrier = pltpu.get_barrier_semaphore()
    greeted = [at_z(d) for d in (1, 2, 3)] + [at_y(d) for d in (1, 2, 3)] + [at_x(p1), at_x(p2), partner]
    for where in greeted:
        pl.semaphore_signal(barrier, inc=1, device_id=where, device_id_type=MESH)
    pl.semaphore_wait(barrier, len(greeted))

    for d in (1, 3, 2):
        go(block_hbm, own_thin, wz_s.at[d], wz_r.at[SIDE - d], at_z(d))

    for d in (1, 3):
        for q in range(SIDE):
            go(tail_hbm.at[owner_rows(d, q)], tbuf.at[SIDE - d, PLACE[q], pl.ds(0, depth)],
               t_s.at[d, PLACE[q]], t_r.at[SIDE - d, PLACE[q]], at_z(d))
    for h in range(2):
        for q in range(SIDE):
            go(tail_hbm.at[owner_rows(2, q), pl.ds(h * lane, lane)], relay.at[h, PLACE[q]],
               r_s.at[h, PLACE[q]], r_r.at[h, PLACE[q]], at_z(step))

    zeros = jnp.zeros((pad - depth, width), F32)
    for j in range(SIDE):
        for q in range(SIDE):
            tbuf[j, q, pl.ds(depth, pad - depth), :] = zeros
    for q in range(SIDE):
        pbuf[q, pl.ds(depth, pad - depth), :] = jnp.zeros((pad - depth, window), F32)

    def thin_rows(zz, yy):
        return wall.at[r, pl.ds(pl.multiple_of((zz * SIDE + yy) * thin, 8), thin)]

    locals_[0].wait()
    for d in (1, 2, 3):
        dst = thin_rows((z + d) % SIDE, y)
        arrived(dst, wz_s.at[d], wz_r.at[d])
    thin_copies = []
    for d in (1, 3, 2):
        for zz in range(SIDE):
            thin_copies.append(go(thin_rows(zz, y), thin_rows(zz, y), wy_s.at[d, zz], wy_r.at[SIDE - d, zz], at_y(d), False))

    def part_rows(i):
        return pl.ds(i * part, part)

    for i in range(PARTS):
        go(panel_hbm.at[part_rows(i)], pbuf.at[2, part_rows(i)], p_s.at[0, i], p_r.at[2, i], at_y(1))
        go(panel_hbm.at[part_rows(i)], pbuf.at[1, part_rows(i)], p_s.at[1, i], p_r.at[1, i], at_y(3))

    for d in (1, 2, 3):
        for zz in range(SIDE):
            arrived(thin_rows(zz, (y + d) % SIDE), wy_s.at[d, zz], wy_r.at[d, zz])
    for copy in thin_copies:
        copy.wait_send()

    diag = rows_of(r, share)
    wall[r, :, diag] = lower_inverse(wall[r, :, diag])
    go(wall.at[r], wall.at[r], wa_s, wa_r, at_x(p2))
    arrived(wall.at[2 * p2 + k], wa_s, wa_r)
    go(wall.at[r], wall.at[r], wb_s.at[0], wb_r.at[0], at_x(p1))
    go(wall.at[2 * p2 + k], wall.at[2 * p2 + k], wb_s.at[1], wb_r.at[1], at_x(p1))
    arrived(wall.at[2 * p1 + k], wb_s.at[0], wb_r.at[0])
    arrived(wall.at[2 * p12 + k], wb_s.at[1], wb_r.at[1])
    for i in range(SIDE):
        go(wall.at[2 * i + k], wall.at[2 * i + k], wc_s.at[i], wc_r.at[i], partner)

    near = 2 - k

    def pass_panel(i):
        arrived(pbuf.at[near, part_rows(i)], p_s.at[2, i], p_r.at[near, i])
        go(pbuf.at[near, part_rows(i)], pbuf.at[3, part_rows(i)], p_s.at[2, i], p_r.at[3, i], at_y(step))

    pass_panel(0)
    for i in range(SIDE):
        arrived(wall.at[2 * i + 1 - k], wc_s.at[i], wc_r.at[i])
    pass_panel(1)

    def clear(i, _):
        inv[rows_of(i), :] = jnp.zeros((128, window), F32)
        return 0

    blocks = window // share
    lax.fori_loop(0, window // 128, clear, 0)
    for i in range(blocks):
        inv[pl.ds(i * share, share), pl.ds(i * share, share)] = wall[i, :, pl.ds(i * share, share)]
    size = share
    while size < window:
        count = size // share
        strip = min(size, 256)
        for base in range(0, window, 2 * size):
            top, low_rows = pl.ds(base, size), pl.ds(base + size, size)

            def below(i, _, base=base, size=size, count=count, strip=strip, top=top, low_rows=low_rows):
                start = pl.multiple_of(i * strip, strip)
                left = inv[pl.ds(base + size + start, strip), low_rows]
                under = wall[pl.ds(base // share + count, count), :, top].reshape(size, size)
                tmp[pl.ds(0, strip), pl.ds(0, size)] = dot(left, under)
                inv[pl.ds(base + size + start, strip), top] = -dot(tmp[pl.ds(0, strip), pl.ds(0, size)], inv[top, top])
                return 0

            if strip == size:
                below(0, 0)
            else:
                lax.fori_loop(0, size // strip, below, 0)
        size *= 2

    def split_inverse(i, _):
        high, rest = halves(inv[rows_of(i), :])
        inv_hi[rows_of(i), :] = high
        inv_lo[rows_of(i), :] = rest
        return 0

    lax.fori_loop(0, window // 128, split_inverse, 0)
    pass_panel(2)

    def turn_panel(q, _):
        def split_rows(i, _):
            high, rest = halves(pbuf[q, rows_of(i), :])
            phi[rows_of(i), :] = high
            plo[rows_of(i), :] = rest
            return 0

        lax.fori_loop(0, pad // 128, split_rows, 0)
        place = pl.ds(pl.multiple_of(q * pad, pad), pad)
        for n in range(0, window, 256):
            deep, cols = pl.ds(n, window - n), pl.ds(n, 256)
            product = (
                mm(phi[:, deep], inv_hi[deep, cols])
                + mm(phi[:, deep], inv_lo[deep, cols])
                + mm(plo[:, deep], inv_hi[deep, cols])
            )
            high, rest = halves(-product.T)
            pthi[cols, place] = high
            ptlo[cols, place] = rest
        return 0

    def panel_here(q):
        for i in range(PARTS):
            arrived(pbuf.at[q, part_rows(i)], p_s.at[0, i], p_r.at[q, i])

    locals_[1].wait()
    for i in range(PARTS):
        arrived(pbuf.at[3 - near, part_rows(i)], p_s.at[0, i], p_r.at[3 - near, i])
    lax.fori_loop(0, 3, turn_panel, 0)

    def take_tail(j, places, cols):
        for q in places:
            high, rest = halves(tbuf[j, q, :, cols])
            thi[pl.ds(q * pad, pad), cols] = high
            tlo[pl.ds(q * pad, pad), cols] = rest

    strip = 512

    def product(j, places, cols, fresh):
        take_tail(j, places, cols)
        deep = pl.ds(places[0] * pad, len(places) * pad)

        def one(i, _):
            rows = rows_of(i, strip)
            total = (
                mm(pthi[rows, deep], thi[deep, cols])
                + mm(pthi[rows, deep], tlo[deep, cols])
                + mm(ptlo[rows, deep], thi[deep, cols])
            )
            for h in range(total.shape[1] // lane):
                u = 2 * j + h + cols.start // lane
                piece = total[:, h * lane:(h + 1) * lane]
                sums[u, rows, :] = piece if fresh else sums[u, rows, :] + piece
            return 0

        lax.fori_loop(0, window // strip, one, 0)

    whole = pl.ds(0, width)
    early = (0, 1, 2)

    def tail_here(j):
        for q in range(SIDE):
            arrived(tbuf.at[j, q, pl.ds(0, depth)], t_s.at[1, q], t_r.at[j, q])

    for copy in locals_[2:]:
        copy.wait()
    product(0, early, whole, True)
    own = dot_t(inv[rows_of(r, share), :], rhs[...])
    for h in range(2):
        sums[h] = sums[h] + own[:, h * lane:(h + 1) * lane]
    tail_here(1)
    product(1, early, whole, True)
    tail_here(3)
    product(3, early, whole, True)

    def pass_tail(h):
        for q in range(SIDE):
            q = PLACE[q]
            arrived(relay.at[h, q], r_s.at[h, q], r_r.at[h, q])
            go(relay.at[h, q], tbuf.at[2, q, pl.ds(0, depth), pl.ds(h * lane, lane)],
               f_s.at[h, q], f_r.at[h, q], at_z(step))

    pass_tail(0)
    panel_here(3)
    turn_panel(3, 0)

    def line(u, rr):
        return sums.at[u, rows_of(rr, share)]

    def to_core(u):
        for i in range(SIDE):
            go(line(u, 2 * i + 1 - k), core_in.at[u, i], c_s.at[u, i], c_r.at[u, i], partner)

    def to_first(u):
        for i in range(SIDE):
            arrived(core_in.at[u, i], c_s.at[u, i], c_r.at[u, i])
            rows = rows_of(2 * i + k, share)
            sums[u, rows, :] = sums[u, rows, :] + core_in[u, i]
        go(line(u, 2 * p1 + k), first_in.at[u, 0], a_s.at[u, 0], a_r.at[u, 0], at_x(p1))
        go(line(u, 2 * p12 + k), first_in.at[u, 1], a_s.at[u, 1], a_r.at[u, 1], at_x(p1))

    def to_second(u):
        for i, other in ((1, p2), (0, x)):
            arrived(first_in.at[u, i], a_s.at[u, i], a_r.at[u, i])
            rows = rows_of(2 * other + k, share)
            sums[u, rows, :] = sums[u, rows, :] + first_in[u, i]
            if i == 1:
                go(line(u, 2 * p2 + k), second_in.at[u], b_s.at[u], b_r.at[u], at_x(p2))

    def to_last(u):
        j, h = u // 2, u % 2
        arrived(second_in.at[u], b_s.at[u], b_r.at[u])
        rows = rows_of(r, share)
        sums[u, rows, :] = sums[u, rows, :] + second_in[u]
        if j:
            go(line(u, r), last_in.at[SIDE - j, h], l_s.at[u], l_r.at[SIDE - j, h], at_z(j))

    def both(stage, j):
        stage(2 * j)
        stage(2 * j + 1)

    late = (3,)
    product(0, late, whole, False)
    both(to_core, 0)
    product(1, late, whole, False)
    both(to_core, 1)
    both(to_first, 0)
    product(3, late, whole, False)
    both(to_core, 3)
    both(to_first, 1)
    both(to_second, 0)
    pass_tail(1)
    both(to_first, 3)
    both(to_second, 1)
    both(to_last, 0)

    def cross_here(h):
        for q in range(SIDE):
            arrived(tbuf.at[2, q, pl.ds(0, depth), pl.ds(h * lane, lane)], f_s.at[h, q], f_r.at[h, q])

    every = (0, 1, 2, 3)
    cross_here(0)
    product(2, every, pl.ds(0, lane), True)
    to_core(4)
    both(to_second, 3)
    both(to_last, 1)
    to_first(4)
    both(to_last, 3)
    cross_here(1)
    product(2, every, pl.ds(lane, lane), True)
    to_core(5)
    to_second(4)
    to_first(5)
    to_last(4)
    to_second(5)
    to_last(5)

    rows = rows_of(r, share)
    for h in range(2):
        total = sums[h, rows, :]
        for d in (1, 3, 2):
            arrived(last_in.at[d, h], l_s.at[2 + h], l_r.at[d, h])
            total = total + last_in[d, h]
        out_ref[:, h * lane:(h + 1) * lane] = total

    for copy in pending:
        copy.wait_send()


def per_device(tail_vectors, lower_panel, window_rhs, window_block):
    columns = tail_vectors.shape[1]
    depth, window = lower_panel.shape
    share = window_rhs.shape[0]
    lane = columns // 2
    pad = -(-depth // 128) * 128
    groups = window // share
    dma = pltpu.SemaphoreType.DMA
    anywhere = pl.BlockSpec(memory_space=pl.ANY)
    return pl.pallas_call(
        kernel,
        out_shape=jax.ShapeDtypeStruct((share, columns), F32),
        in_specs=[anywhere] * 4,
        out_specs=pl.BlockSpec(memory_space=pltpu.VMEM),
        scratch_shapes=[
            pltpu.VMEM((SIDE, SIDE, pad, columns), F32),
            pltpu.VMEM((2, SIDE, depth, lane), F32),
            pltpu.VMEM((SIDE, pad, window), F32),
            pltpu.VMEM((pad, window), BF16),
            pltpu.VMEM((pad, window), BF16),
            pltpu.VMEM((window, SIDE * pad), BF16),
            pltpu.VMEM((window, SIDE * pad), BF16),
            pltpu.VMEM((groups, share, window), F32),
            pltpu.VMEM((window, window), F32),
            pltpu.VMEM((window, window), BF16),
            pltpu.VMEM((window, window), BF16),
            pltpu.VMEM((256, window // 2), F32),
            pltpu.VMEM((share, columns), F32),
            pltpu.VMEM((SIDE * pad, columns), BF16),
            pltpu.VMEM((SIDE * pad, columns), BF16),
            pltpu.VMEM((2 * SIDE, window, lane), F32),
            pltpu.VMEM((2 * SIDE, SIDE, share, lane), F32),
            pltpu.VMEM((2 * SIDE, 2, share, lane), F32),
            pltpu.VMEM((2 * SIDE, share, lane), F32),
            pltpu.VMEM((SIDE, 2, share, lane), F32),
            dma((7,)),
            dma((SIDE,)), dma((SIDE,)), dma((SIDE, SIDE)), dma((SIDE, SIDE)),
            dma, dma, dma((2,)), dma((2,)), dma((SIDE,)), dma((SIDE,)),
            dma((3, PARTS)), dma((SIDE, PARTS)),
            dma((SIDE, SIDE)), dma((SIDE, SIDE)),
            dma((2, SIDE)), dma((2, SIDE)), dma((2, SIDE)), dma((2, SIDE)),
            dma((2 * SIDE, SIDE)), dma((2 * SIDE, SIDE)),
            dma((2 * SIDE, 2)), dma((2 * SIDE, 2)),
            dma((2 * SIDE,)), dma((2 * SIDE,)),
            dma((2 * SIDE,)), dma((SIDE, 2)),
        ],
        compiler_params=pltpu.CompilerParams(
            collective_id=0, has_side_effects=True, vmem_limit_bytes=65000 * 1024
        ),
    )(tail_vectors, lower_panel, window_block, window_rhs)


def solution(mesh):
    in_specs = (P("row", "col"), P(("row", "col"), None), P("row", "col"), P(("row", "col"), None))
    out_specs = P("row", "col")
    return jax.shard_map(per_device, mesh=mesh, in_specs=in_specs, out_specs=out_specs, check_vma=False)
```

profile of v0, /device:TPU:1, one launch (start us, length us, event | category | flops | bytes accessed | tf_op | source)
XLA Modules:
  0.0 129.9 jit_solution(5560394790522513549)
XLA Ops:
  0.0 128.3 %shard_map.46 = f32[128,256]{1,0:T(8,128)} custom-call(f32[8064,256]{1,0:T(8,128)} %tail_hbm.1, f32[504,1024]{1,0:T(8,128)} %panel_hbm.1, f32[8,1024]{1,0:T(8,128)} %block_hbm.1, f32[128,256]{1,0:T(8,128)} %rhs_hbm.1), custom_call_target="tpu_custom_call" | custom-call | tf_op jit(solution)/shard_map/pallas_call | solution.py:417
  128.3 1.6 %copy.6 = f32[128,256]{1,0:T(8,128)} copy(f32[128,256]{1,0:T(8,128)} %shard_map.46) | data formatting | bytes 262144
where the time goes:
time: 130 us
  Pallas kernels  128 us (98%)
  local copies, waits for them, and re-layouts  1.57 us (1%)
    pallas_call x1, Pallas kernels, per_device(): pl.pallas_call(kernel, out_shape=jax.ShapeDtypeStruct((share, columns), F...  128 us

commit v1 on v0

--- a/solution.py
+++ b/solution.py
@@ -13,7 +13,8 @@
 BF16 = jnp.bfloat16
 SIDE = 4
 PLACE = (0, 1, 3, 2)
-PARTS = 3
+CUTS = (3, 5, 11, 11, 11, 11, 11)
+PARTS = len(CUTS)
 
 
 def dot(a, b):
@@ -69,7 +70,7 @@
     share, width = rhs_hbm.shape
     lane = width // 2
     pad = pbuf.shape[1]
-    part = depth // PARTS
+    unit = depth // sum(CUTS)
     r = lax.axis_index("row")
     c = lax.axis_index("col")
     x, k = r // 2, r % 2
@@ -79,6 +80,10 @@
     p1 = k * mirror + (1 - k) * low
     p2 = k * low + (1 - k) * mirror
     p12 = (x + 2) % SIDE
+    low, mirror = y + 1 - 2 * (y % 2), SIDE - 1 - y
+    q1 = k * mirror + (1 - k) * low
+    q2 = k * low + (1 - k) * mirror
+    q12 = (y + 2) % SIDE
 
     def at_z(d):
         return {"col": ((z + d + SIDE) % SIDE) * SIDE + y}
@@ -127,22 +132,30 @@
         copy.start()
 
     barrier = pltpu.get_barrier_semaphore()
-    greeted = [at_z(d) for d in (1, 2, 3)] + [at_y(d) for d in (1, 2, 3)] + [at_x(p1), at_x(p2), partner]
+    greeted = [at_z(d) for d in (1, 2, 3)] + [at_y(1), at_y(3)] + [at_x(p1), at_x(p2), partner]
     for where in greeted:
         pl.semaphore_signal(barrier, inc=1, device_id=where, device_id_type=MESH)
     pl.semaphore_wait(barrier, len(greeted))
 
-    for d in (1, 3, 2):
+    def part_rows(i):
+        return pl.ds(sum(CUTS[:i]) * unit, CUTS[i] * unit)
+
+    def send_panel(i):
+        go(panel_hbm.at[part_rows(i)], pbuf.at[2, part_rows(i)], p_s.at[0, i], p_r.at[2, i], at_y(1))
+        go(panel_hbm.at[part_rows(i)], pbuf.at[1, part_rows(i)], p_s.at[1, i], p_r.at[1, i], at_y(3))
+
+    for d in (2, 1, 3):
         go(block_hbm, own_thin, wz_s.at[d], wz_r.at[SIDE - d], at_z(d))
-
+    send_panel(0)
+
+    for h in range(2):
+        for q in (0, 1, 3, 2):
+            go(tail_hbm.at[owner_rows(2, q), pl.ds(h * lane, lane)], relay.at[h, PLACE[q]],
+               r_s.at[h, PLACE[q]], r_r.at[h, PLACE[q]], at_z(step))
     for d in (1, 3):
         for q in range(SIDE):
             go(tail_hbm.at[owner_rows(d, q)], tbuf.at[SIDE - d, PLACE[q], pl.ds(0, depth)],
                t_s.at[d, PLACE[q]], t_r.at[SIDE - d, PLACE[q]], at_z(d))
-    for h in range(2):
-        for q in range(SIDE):
-            go(tail_hbm.at[owner_rows(2, q), pl.ds(h * lane, lane)], relay.at[h, PLACE[q]],
-               r_s.at[h, PLACE[q]], r_r.at[h, PLACE[q]], at_z(step))
 
     zeros = jnp.zeros((pad - depth, width), F32)
     for j in range(SIDE):
@@ -154,49 +167,65 @@
     def thin_rows(zz, yy):
         return wall.at[r, pl.ds(pl.multiple_of((zz * SIDE + yy) * thin, 8), thin)]
 
+    def here_y(other):
+        return {"col": z * SIDE + other}
+
     locals_[0].wait()
-    for d in (1, 2, 3):
+    for d in (1, 3, 2):
         dst = thin_rows((z + d) % SIDE, y)
         arrived(dst, wz_s.at[d], wz_r.at[d])
     thin_copies = []
-    for d in (1, 3, 2):
+
+    def swap_thin(sem, mine, where):
         for zz in range(SIDE):
-            thin_copies.append(go(thin_rows(zz, y), thin_rows(zz, y), wy_s.at[d, zz], wy_r.at[SIDE - d, zz], at_y(d), False))
-
-    def part_rows(i):
-        return pl.ds(i * part, part)
-
-    for i in range(PARTS):
-        go(panel_hbm.at[part_rows(i)], pbuf.at[2, part_rows(i)], p_s.at[0, i], p_r.at[2, i], at_y(1))
-        go(panel_hbm.at[part_rows(i)], pbuf.at[1, part_rows(i)], p_s.at[1, i], p_r.at[1, i], at_y(3))
-
-    for d in (1, 2, 3):
+            thin_copies.append(
+                go(thin_rows(zz, mine), thin_rows(zz, mine), wy_s.at[sem, zz], wy_r.at[sem, zz], here_y(where), False)
+            )
+
+    def thin_here(sem, theirs):
         for zz in range(SIDE):
-            arrived(thin_rows(zz, (y + d) % SIDE), wy_s.at[d, zz], wy_r.at[d, zz])
+            arrived(thin_rows(zz, theirs), wy_s.at[sem, zz], wy_r.at[sem, zz])
+
+    swap_thin(0, y, q1)
+    send_panel(1)
+    thin_here(0, q1)
+    swap_thin(1, y, q2)
+    swap_thin(2, q1, q2)
+    for i in range(2, PARTS):
+        send_panel(i)
+    thin_here(1, q2)
+    thin_here(2, q12)
     for copy in thin_copies:
         copy.wait_send()
 
     diag = rows_of(r, share)
     wall[r, :, diag] = lower_inverse(wall[r, :, diag])
-    go(wall.at[r], wall.at[r], wa_s, wa_r, at_x(p2))
-    arrived(wall.at[2 * p2 + k], wa_s, wa_r)
-    go(wall.at[r], wall.at[r], wb_s.at[0], wb_r.at[0], at_x(p1))
-    go(wall.at[2 * p2 + k], wall.at[2 * p2 + k], wb_s.at[1], wb_r.at[1], at_x(p1))
-    arrived(wall.at[2 * p1 + k], wb_s.at[0], wb_r.at[0])
-    arrived(wall.at[2 * p12 + k], wb_s.at[1], wb_r.at[1])
-    for i in range(SIDE):
-        go(wall.at[2 * i + k], wall.at[2 * i + k], wc_s.at[i], wc_r.at[i], partner)
-
     near = 2 - k
 
     def pass_panel(i):
         arrived(pbuf.at[near, part_rows(i)], p_s.at[2, i], p_r.at[near, i])
         go(pbuf.at[near, part_rows(i)], pbuf.at[3, part_rows(i)], p_s.at[2, i], p_r.at[3, i], at_y(step))
 
+    def strip_to_core(i, other):
+        go(wall.at[2 * other + k], wall.at[2 * other + k], wc_s.at[i], wc_r.at[i], partner)
+
+    go(wall.at[r], wall.at[r], wa_s, wa_r, at_x(p2))
+    go(wall.at[r], wall.at[r], wb_s.at[0], wb_r.at[0], at_x(p1))
+    strip_to_core(0, x)
     pass_panel(0)
-    for i in range(SIDE):
-        arrived(wall.at[2 * i + 1 - k], wc_s.at[i], wc_r.at[i])
     pass_panel(1)
+    arrived(wall.at[2 * p2 + k], wa_s, wa_r)
+    go(wall.at[2 * p2 + k], wall.at[2 * p2 + k], wb_s.at[1], wb_r.at[1], at_x(p1))
+    strip_to_core(1, p2)
+    arrived(wall.at[2 * p1 + k], wb_s.at[0], wb_r.at[0])
+    strip_to_core(2, p1)
+    pass_panel(2)
+    pass_panel(3)
+    arrived(wall.at[2 * p12 + k], wb_s.at[1], wb_r.at[1])
+    strip_to_core(3, p12)
+    pass_panel(4)
+    for i, other in enumerate((x, p1, p2, p12)):
+        arrived(wall.at[2 * other + 1 - k], wc_s.at[i], wc_r.at[i])
 
     def clear(i, _):
         inv[rows_of(i), :] = jnp.zeros((128, window), F32)
@@ -234,7 +263,12 @@
         return 0
 
     lax.fori_loop(0, window // 128, split_inverse, 0)
-    pass_panel(2)
+
+    def pass_tail(h):
+        for q in range(SIDE):
+            arrived(relay.at[h, q], r_s.at[h, q], r_r.at[h, q])
+            go(relay.at[h, q], tbuf.at[2, q, pl.ds(0, depth), pl.ds(h * lane, lane)],
+               f_s.at[h, q], f_r.at[h, q], at_z(step))
 
     def turn_panel(q, _):
         def split_rows(i, _):
@@ -262,9 +296,14 @@
             arrived(pbuf.at[q, part_rows(i)], p_s.at[0, i], p_r.at[q, i])
 
     locals_[1].wait()
+    turn_panel(0, 0)
+    pass_panel(5)
+    pass_panel(6)
+    pass_tail(0)
     for i in range(PARTS):
         arrived(pbuf.at[3 - near, part_rows(i)], p_s.at[0, i], p_r.at[3 - near, i])
-    lax.fori_loop(0, 3, turn_panel, 0)
+    lax.fori_loop(1, 3, turn_panel, 0)
+    pass_tail(1)
 
     def take_tail(j, places, cols):
         for q in places:
@@ -296,29 +335,21 @@
     whole = pl.ds(0, width)
     early = (0, 1, 2)
 
-    def tail_here(j):
-        for q in range(SIDE):
+    def tail_here(j, places):
+        for q in places:
             arrived(tbuf.at[j, q, pl.ds(0, depth)], t_s.at[1, q], t_r.at[j, q])
 
+    late = (3,)
     for copy in locals_[2:]:
         copy.wait()
     product(0, early, whole, True)
     own = dot_t(inv[rows_of(r, share), :], rhs[...])
     for h in range(2):
         sums[h] = sums[h] + own[:, h * lane:(h + 1) * lane]
-    tail_here(1)
-    product(1, early, whole, True)
-    tail_here(3)
-    product(3, early, whole, True)
-
-    def pass_tail(h):
-        for q in range(SIDE):
-            q = PLACE[q]
-            arrived(relay.at[h, q], r_s.at[h, q], r_r.at[h, q])
-            go(relay.at[h, q], tbuf.at[2, q, pl.ds(0, depth), pl.ds(h * lane, lane)],
-               f_s.at[h, q], f_r.at[h, q], at_z(step))
-
-    pass_tail(0)
+    for j in (1 + 2 * k, 3 - 2 * k):
+        tail_here(j, early)
+        product(j, early, whole, True)
+
     panel_here(3)
     turn_panel(3, 0)
 
@@ -357,37 +388,37 @@
         stage(2 * j)
         stage(2 * j + 1)
 
-    late = (3,)
+    def cross(h, places, fresh):
+        for q in places:
+            arrived(tbuf.at[2, q, pl.ds(0, depth), pl.ds(h * lane, lane)], f_s.at[h, q], f_r.at[h, q])
+        product(2, places, pl.ds(h * lane, lane), fresh)
+
     product(0, late, whole, False)
     both(to_core, 0)
+    tail_here(1, late)
     product(1, late, whole, False)
     both(to_core, 1)
     both(to_first, 0)
+    tail_here(3, late)
     product(3, late, whole, False)
     both(to_core, 3)
     both(to_first, 1)
+    cross(0, (0, 1), True)
+    both(to_first, 3)
     both(to_second, 0)
-    pass_tail(1)
-    both(to_first, 3)
+    cross(0, (2, 3), False)
+    to_core(4)
     both(to_second, 1)
+    to_first(4)
+    cross(1, (0, 1), True)
     both(to_last, 0)
-
-    def cross_here(h):
-        for q in range(SIDE):
-            arrived(tbuf.at[2, q, pl.ds(0, depth), pl.ds(h * lane, lane)], f_s.at[h, q], f_r.at[h, q])
-
-    every = (0, 1, 2, 3)
-    cross_here(0)
-    product(2, every, pl.ds(0, lane), True)
-    to_core(4)
     both(to_second, 3)
     both(to_last, 1)
-    to_first(4)
+    cross(1, (2,), False)
+    to_second(4)
     both(to_last, 3)
-    cross_here(1)
-    product(2, every, pl.ds(lane, lane), True)
+    cross(1, (3,), False)
     to_core(5)
-    to_second(4)
     to_first(5)
     to_last(4)
     to_second(5)
@@ -441,7 +472,7 @@
             pltpu.VMEM((2 * SIDE, share, lane), F32),
             pltpu.VMEM((SIDE, 2, share, lane), F32),
             dma((7,)),
-            dma((SIDE,)), dma((SIDE,)), dma((SIDE, SIDE)), dma((SIDE, SIDE)),
+            dma((SIDE,)), dma((SIDE,)), dma((3, SIDE)), dma((3, SIDE)),
             dma, dma, dma((2,)), dma((2,)), dma((SIDE,)), dma((SIDE,)),
             dma((3, PARTS)), dma((SIDE, PARTS)),
             dma((SIDE, SIDE)), dma((SIDE, SIDE)),

time: 130 us -> 121 us (0.931)
  Pallas kernels: 128 us -> 119 us
    pallas_call x1, Pallas kernels: 128 us -> 119 us  [per_device(): pl.pallas_call(kernel, out_shape=jax.ShapeDtypeStruct((share, columns), F...]
where the time goes in v1:
time: 121 us
  Pallas kernels  119 us (98%)
  local copies, waits for them, and re-layouts  1.57 us (1%)
    pallas_call x1, Pallas kernels, per_device(): pl.pallas_call(kernel, out_shape=jax.ShapeDtypeStruct((share, columns), F...  119 us

profile of v1, /device:TPU:1, one launch (start us, length us, event | category | flops | bytes accessed | tf_op | source)
XLA Modules:
  0.0 120.9 jit_solution(8044348639575185765)
XLA Ops:
  0.0 119.3 %shard_map.46 = f32[128,256]{1,0:T(8,128)} custom-call(f32[8064,256]{1,0:T(8,128)} %tail_hbm.1, f32[504,1024]{1,0:T(8,128)} %panel_hbm.1, f32[8,1024]{1,0:T(8,128)} %block_hbm.1, f32[128,256]{1,0:T(8,128)} %rhs_hbm.1), custom_call_target="tpu_custom_call" | custom-call | tf_op jit(solution)/shard_map/pallas_call | solution.py:448
  119.3 1.6 %copy.6 = f32[128,256]{1,0:T(8,128)} copy(f32[128,256]{1,0:T(8,128)} %shard_map.46) | data formatting | bytes 262144

commit v2 on v1

--- a/solution.py
+++ b/solution.py
@@ -13,16 +13,17 @@
 BF16 = jnp.bfloat16
 SIDE = 4
 PLACE = (0, 1, 3, 2)
-CUTS = (3, 5, 11, 11, 11, 11, 11)
+CUTS = (9, 6, 8, 8, 8, 12, 12)
 PARTS = len(CUTS)
+FORTH = 4
 
 
 def dot(a, b):
     return jnp.dot(a, b, precision=HIGHEST, preferred_element_type=F32)
 
 
-def dot_t(a, b):
-    return lax.dot_general(a, b, (((0,), (0,)), ((), ())), precision=HIGHEST, preferred_element_type=F32)
+def mm_t(a, b):
+    return lax.dot_general(a, b, (((0,), (0,)), ((), ())), preferred_element_type=F32)
 
 
 def mm(a, b):
@@ -75,26 +76,26 @@
     c = lax.axis_index("col")
     x, k = r // 2, r % 2
     z, y = c // SIDE, c % SIDE
-    step = 1 - 2 * k
     low, mirror = x + 1 - 2 * (x % 2), SIDE - 1 - x
     p1 = k * mirror + (1 - k) * low
     p2 = k * low + (1 - k) * mirror
     p12 = (x + 2) % SIDE
-    low, mirror = y + 1 - 2 * (y % 2), SIDE - 1 - y
-    q1 = k * mirror + (1 - k) * low
-    q2 = k * low + (1 - k) * mirror
-    q12 = (y + 2) % SIDE
-
-    def at_z(d):
-        return {"col": ((z + d + SIDE) % SIDE) * SIDE + y}
-
-    def at_y(d):
-        return {"col": z * SIDE + (y + d + SIDE) % SIDE}
+
+    def place_at(dt, dp):
+        zz = (z + dt * (1 - k) + dp * k + 2 * SIDE) % SIDE
+        yy = (y + dt * k + dp * (1 - k) + 2 * SIDE) % SIDE
+        return zz * SIDE + yy
+
+    def at_t(d):
+        return {"row": r, "col": place_at(d, 0)}
+
+    def at_p(d):
+        return {"row": r, "col": place_at(0, d)}
 
     def at_x(other):
-        return {"row": 2 * other + k}
-
-    partner = {"row": 2 * x + 1 - k}
+        return {"row": 2 * other + k, "col": c}
+
+    partner = {"row": 2 * x + 1 - k, "col": c}
     pending = []
 
     def remote(src, dst, send, recv, where):
@@ -112,9 +113,8 @@
     def arrived(dst, send, recv):
         remote(dst, dst, send, recv, partner).wait_recv()
 
-    def owner_rows(dz, dy):
-        owner = ((z + dz + SIDE) % SIDE) * SIDE + (y + dy) % SIDE
-        return pl.ds(pl.multiple_of(owner * depth, 8), depth)
+    def owner_rows(dt, dp):
+        return pl.ds(pl.multiple_of(place_at(dt, dp) * depth, 8), depth)
 
     def rows_of(index, size=128):
         return pl.ds(pl.multiple_of(index * size, size), size)
@@ -132,7 +132,10 @@
         copy.start()
 
     barrier = pltpu.get_barrier_semaphore()
-    greeted = [at_z(d) for d in (1, 2, 3)] + [at_y(1), at_y(3)] + [at_x(p1), at_x(p2), partner]
+    greeted = [at_x(p1), at_x(p2), partner] + [
+        {"row": 2 * x + core, "col": place_at(*offset)}
+        for core in range(2) for d in (1, 2, 3) for offset in ((d, 0), (0, d))
+    ]
     for where in greeted:
         pl.semaphore_signal(barrier, inc=1, device_id=where, device_id_type=MESH)
     pl.semaphore_wait(barrier, len(greeted))
@@ -141,22 +144,18 @@
         return pl.ds(sum(CUTS[:i]) * unit, CUTS[i] * unit)
 
     def send_panel(i):
-        go(panel_hbm.at[part_rows(i)], pbuf.at[2, part_rows(i)], p_s.at[0, i], p_r.at[2, i], at_y(1))
-        go(panel_hbm.at[part_rows(i)], pbuf.at[1, part_rows(i)], p_s.at[1, i], p_r.at[1, i], at_y(3))
+        go(panel_hbm.at[part_rows(i)], pbuf.at[2, part_rows(i)], p_s.at[0, i], p_r.at[2, i], at_p(1))
+        go(panel_hbm.at[part_rows(i)], pbuf.at[1, part_rows(i)], p_s.at[1, i], p_r.at[1, i], at_p(3))
 
     for d in (2, 1, 3):
-        go(block_hbm, own_thin, wz_s.at[d], wz_r.at[SIDE - d], at_z(d))
+        go(block_hbm, own_thin, wz_s.at[d], wz_r.at[SIDE - d], at_t(d))
     send_panel(0)
 
-    for h in range(2):
-        for q in (0, 1, 3, 2):
-            go(tail_hbm.at[owner_rows(2, q), pl.ds(h * lane, lane)], relay.at[h, PLACE[q]],
-               r_s.at[h, PLACE[q]], r_r.at[h, PLACE[q]], at_z(step))
-    for d in (1, 3):
-        for q in range(SIDE):
-            go(tail_hbm.at[owner_rows(d, q)], tbuf.at[SIDE - d, PLACE[q], pl.ds(0, depth)],
-               t_s.at[d, PLACE[q]], t_r.at[SIDE - d, PLACE[q]], at_z(d))
-
+    def clear(i, _):
+        inv[rows_of(i), :] = jnp.zeros((128, window), F32)
+        return 0
+
+    lax.fori_loop(0, window // 128, clear, 0)
     zeros = jnp.zeros((pad - depth, width), F32)
     for j in range(SIDE):
         for q in range(SIDE):
@@ -164,47 +163,47 @@
     for q in range(SIDE):
         pbuf[q, pl.ds(depth, pad - depth), :] = jnp.zeros((pad - depth, window), F32)
 
-    def thin_rows(zz, yy):
-        return wall.at[r, pl.ds(pl.multiple_of((zz * SIDE + yy) * thin, 8), thin)]
-
-    def here_y(other):
-        return {"col": z * SIDE + other}
+    def thin_rows(dt, dp):
+        return wall.at[r, pl.ds(pl.multiple_of(place_at(dt, dp) * thin, 8), thin)]
 
     locals_[0].wait()
     for d in (1, 3, 2):
-        dst = thin_rows((z + d) % SIDE, y)
-        arrived(dst, wz_s.at[d], wz_r.at[d])
+        arrived(thin_rows(d, 0), wz_s.at[d], wz_r.at[d])
     thin_copies = []
+    pc = k * z + (1 - k) * y
+    near = 1 - 2 * (pc % 2)
 
     def swap_thin(sem, mine, where):
-        for zz in range(SIDE):
+        for d in range(SIDE):
             thin_copies.append(
-                go(thin_rows(zz, mine), thin_rows(zz, mine), wy_s.at[sem, zz], wy_r.at[sem, zz], here_y(where), False)
+                go(thin_rows(d, mine), thin_rows(d, mine), wy_s.at[sem, d], wy_r.at[sem, d], at_p(where), False)
             )
 
     def thin_here(sem, theirs):
-        for zz in range(SIDE):
-            arrived(thin_rows(zz, theirs), wy_s.at[sem, zz], wy_r.at[sem, zz])
-
-    swap_thin(0, y, q1)
+        for d in range(SIDE):
+            arrived(thin_rows(d, theirs), wy_s.at[sem, d], wy_r.at[sem, d])
+
+    swap_thin(0, 0, near)
     send_panel(1)
-    thin_here(0, q1)
-    swap_thin(1, y, q2)
-    swap_thin(2, q1, q2)
+    thin_here(0, near)
+    swap_thin(1, 0, -near)
+    swap_thin(2, near, -near)
     for i in range(2, PARTS):
         send_panel(i)
-    thin_here(1, q2)
-    thin_here(2, q12)
+    thin_here(1, -near)
+    thin_here(2, 2)
     for copy in thin_copies:
         copy.wait_send()
 
     diag = rows_of(r, share)
     wall[r, :, diag] = lower_inverse(wall[r, :, diag])
-    near = 2 - k
+    def came_from(i):
+        return 2 if i < FORTH else 1
 
     def pass_panel(i):
-        arrived(pbuf.at[near, part_rows(i)], p_s.at[2, i], p_r.at[near, i])
-        go(pbuf.at[near, part_rows(i)], pbuf.at[3, part_rows(i)], p_s.at[2, i], p_r.at[3, i], at_y(step))
+        side = came_from(i)
+        arrived(pbuf.at[side, part_rows(i)], p_s.at[2, i], p_r.at[side, i])
+        go(pbuf.at[side, part_rows(i)], pbuf.at[3, part_rows(i)], p_s.at[2, i], p_r.at[3, i], at_p(2 * side - 3))
 
     def strip_to_core(i, other):
         go(wall.at[2 * other + k], wall.at[2 * other + k], wc_s.at[i], wc_r.at[i], partner)
@@ -212,27 +211,32 @@
     go(wall.at[r], wall.at[r], wa_s, wa_r, at_x(p2))
     go(wall.at[r], wall.at[r], wb_s.at[0], wb_r.at[0], at_x(p1))
     strip_to_core(0, x)
-    pass_panel(0)
-    pass_panel(1)
+    for i in range(FORTH):
+        pass_panel(i)
     arrived(wall.at[2 * p2 + k], wa_s, wa_r)
     go(wall.at[2 * p2 + k], wall.at[2 * p2 + k], wb_s.at[1], wb_r.at[1], at_x(p1))
     strip_to_core(1, p2)
+    for i in range(FORTH, PARTS):
+        pass_panel(i)
+
+    for q in (0, 1, 3, 2):
+        for d in (1, 3):
+            go(tail_hbm.at[owner_rows(d, q)], tbuf.at[SIDE - d, PLACE[q], pl.ds(0, depth)],
+               t_s.at[d, PLACE[q]], t_r.at[SIDE - d, PLACE[q]], at_t(d))
+    for h in range(2):
+        for q in (0, 1, 3, 2):
+            go(tail_hbm.at[owner_rows(2, q), pl.ds(h * lane, lane)], relay.at[h, PLACE[q]],
+               r_s.at[h, PLACE[q]], r_r.at[h, PLACE[q]], at_t(1 + 2 * (PLACE[q] % 2)))
+
     arrived(wall.at[2 * p1 + k], wb_s.at[0], wb_r.at[0])
     strip_to_core(2, p1)
-    pass_panel(2)
-    pass_panel(3)
     arrived(wall.at[2 * p12 + k], wb_s.at[1], wb_r.at[1])
     strip_to_core(3, p12)
-    pass_panel(4)
+
     for i, other in enumerate((x, p1, p2, p12)):
         arrived(wall.at[2 * other + 1 - k], wc_s.at[i], wc_r.at[i])
 
-    def clear(i, _):
-        inv[rows_of(i), :] = jnp.zeros((128, window), F32)
-        return 0
-
     blocks = window // share
-    lax.fori_loop(0, window // 128, clear, 0)
     for i in range(blocks):
         inv[pl.ds(i * share, share), pl.ds(i * share, share)] = wall[i, :, pl.ds(i * share, share)]
     size = share
@@ -268,7 +272,7 @@
         for q in range(SIDE):
             arrived(relay.at[h, q], r_s.at[h, q], r_r.at[h, q])
             go(relay.at[h, q], tbuf.at[2, q, pl.ds(0, depth), pl.ds(h * lane, lane)],
-               f_s.at[h, q], f_r.at[h, q], at_z(step))
+               f_s.at[h, q], f_r.at[h, q], at_t(1 + 2 * (q % 2)))
 
     def turn_panel(q, _):
         def split_rows(i, _):
@@ -293,17 +297,13 @@
 
     def panel_here(q):
         for i in range(PARTS):
-            arrived(pbuf.at[q, part_rows(i)], p_s.at[0, i], p_r.at[q, i])
+            if q != came_from(i):
+                arrived(pbuf.at[q, part_rows(i)], p_s.at[0, i], p_r.at[q, i])
 
     locals_[1].wait()
-    turn_panel(0, 0)
-    pass_panel(5)
-    pass_panel(6)
-    pass_tail(0)
-    for i in range(PARTS):
-        arrived(pbuf.at[3 - near, part_rows(i)], p_s.at[0, i], p_r.at[3 - near, i])
-    lax.fori_loop(1, 3, turn_panel, 0)
-    pass_tail(1)
+    panel_here(1)
+    panel_here(2)
+    lax.fori_loop(0, 3, turn_panel, 0)
 
     def take_tail(j, places, cols):
         for q in places:
@@ -333,103 +333,101 @@
         lax.fori_loop(0, window // strip, one, 0)
 
     whole = pl.ds(0, width)
-    early = (0, 1, 2)
-
-    def tail_here(j, places):
+    def beside(j, places, fresh):
         for q in places:
             arrived(tbuf.at[j, q, pl.ds(0, depth)], t_s.at[1, q], t_r.at[j, q])
-
-    late = (3,)
-    for copy in locals_[2:]:
-        copy.wait()
-    product(0, early, whole, True)
-    own = dot_t(inv[rows_of(r, share), :], rhs[...])
-    for h in range(2):
-        sums[h] = sums[h] + own[:, h * lane:(h + 1) * lane]
-    for j in (1 + 2 * k, 3 - 2 * k):
-        tail_here(j, early)
-        product(j, early, whole, True)
-
-    panel_here(3)
-    turn_panel(3, 0)
-
-    def line(u, rr):
-        return sums.at[u, rows_of(rr, share)]
-
-    def to_core(u):
-        for i in range(SIDE):
-            go(line(u, 2 * i + 1 - k), core_in.at[u, i], c_s.at[u, i], c_r.at[u, i], partner)
-
-    def to_first(u):
-        for i in range(SIDE):
-            arrived(core_in.at[u, i], c_s.at[u, i], c_r.at[u, i])
-            rows = rows_of(2 * i + k, share)
-            sums[u, rows, :] = sums[u, rows, :] + core_in[u, i]
-        go(line(u, 2 * p1 + k), first_in.at[u, 0], a_s.at[u, 0], a_r.at[u, 0], at_x(p1))
-        go(line(u, 2 * p12 + k), first_in.at[u, 1], a_s.at[u, 1], a_r.at[u, 1], at_x(p1))
-
-    def to_second(u):
-        for i, other in ((1, p2), (0, x)):
-            arrived(first_in.at[u, i], a_s.at[u, i], a_r.at[u, i])
-            rows = rows_of(2 * other + k, share)
-            sums[u, rows, :] = sums[u, rows, :] + first_in[u, i]
-            if i == 1:
-                go(line(u, 2 * p2 + k), second_in.at[u], b_s.at[u], b_r.at[u], at_x(p2))
-
-    def to_last(u):
-        j, h = u // 2, u % 2
-        arrived(second_in.at[u], b_s.at[u], b_r.at[u])
-        rows = rows_of(r, share)
-        sums[u, rows, :] = sums[u, rows, :] + second_in[u]
-        if j:
-            go(line(u, r), last_in.at[SIDE - j, h], l_s.at[u], l_r.at[SIDE - j, h], at_z(j))
-
-    def both(stage, j):
-        stage(2 * j)
-        stage(2 * j + 1)
+        product(j, places, whole, fresh)
 
     def cross(h, places, fresh):
         for q in places:
             arrived(tbuf.at[2, q, pl.ds(0, depth), pl.ds(h * lane, lane)], f_s.at[h, q], f_r.at[h, q])
         product(2, places, pl.ds(h * lane, lane), fresh)
 
-    product(0, late, whole, False)
+    def lines(u, xx):
+        return rows_of(xx, 2 * share) if u > 1 else rows_of(2 * xx + k, share)
+
+    def height(u):
+        return pl.ds(0, 2 * share if u > 1 else share)
+
+    def to_core(u):
+        for i in range(SIDE):
+            go(sums.at[u, rows_of(2 * i + 1 - k, share)], core_in.at[u, i], c_s.at[u, i], c_r.at[u, i], partner)
+
+    def to_first(u):
+        if u < 2:
+            for i in range(SIDE):
+                arrived(core_in.at[u, i], c_s.at[u, i], c_r.at[u, i])
+                rows = rows_of(2 * i + k, share)
+                sums[u, rows, :] = sums[u, rows, :] + core_in[u, i]
+        for i, other in ((1, p12), (0, p1)):
+            go(sums.at[u, lines(u, other)], first_in.at[u, i, height(u)], a_s.at[u, i], a_r.at[u, i], at_x(p1))
+
+    def to_second(u):
+        for i, other in ((1, p2), (0, x)):
+            arrived(first_in.at[u, i, height(u)], a_s.at[u, i], a_r.at[u, i])
+            rows = lines(u, other)
+            sums[u, rows, :] = sums[u, rows, :] + first_in[u, i, height(u), :]
+            if i == 1:
+                go(sums.at[u, rows], second_in.at[u, height(u)], b_s.at[u], b_r.at[u], at_x(p2))
+
+    def to_last(u):
+        j, h = u // 2, u % 2
+        arrived(second_in.at[u, height(u)], b_s.at[u], b_r.at[u])
+        rows = lines(u, x)
+        sums[u, rows, :] = sums[u, rows, :] + second_in[u, height(u), :]
+        if j:
+            for i, core in enumerate((k, 1 - k)):
+                go(sums.at[u, rows_of(2 * x + core, share)], last_in.at[k, SIDE - j, h],
+                   l_s.at[i, u], l_r.at[k, SIDE - j, h], {"row": 2 * x + core, "col": place_at(j, 0)})
+
+    def both(stage, j):
+        stage(2 * j)
+        stage(2 * j + 1)
+
+    for copy in locals_[2:]:
+        copy.wait()
+    product(0, (0, 1, 2), whole, True)
+    rhs_hi, rhs_lo = halves(rhs[...])
+    own_hi, own_lo = inv_hi[rows_of(r, share), :], inv_lo[rows_of(r, share), :]
+    own = mm_t(own_hi, rhs_hi) + mm_t(own_hi, rhs_lo) + mm_t(own_lo, rhs_hi)
+    for h in range(2):
+        sums[h] = sums[h] + own[:, h * lane:(h + 1) * lane]
+    panel_here(3)
+    turn_panel(3, 0)
+    product(0, (3,), whole, False)
     both(to_core, 0)
-    tail_here(1, late)
-    product(1, late, whole, False)
-    both(to_core, 1)
+    beside(1, (0, 1), True)
     both(to_first, 0)
-    tail_here(3, late)
-    product(3, late, whole, False)
-    both(to_core, 3)
+    beside(3, (0, 1), True)
+    beside(1, (2, 3), False)
     both(to_first, 1)
-    cross(0, (0, 1), True)
+    beside(3, (2, 3), False)
     both(to_first, 3)
     both(to_second, 0)
+    pass_tail(0)
+    pass_tail(1)
+    both(to_last, 0)
+    both(to_second, 1)
+    cross(0, (0, 1), True)
     cross(0, (2, 3), False)
-    to_core(4)
-    both(to_second, 1)
     to_first(4)
+    both(to_last, 1)
     cross(1, (0, 1), True)
-    both(to_last, 0)
     both(to_second, 3)
-    both(to_last, 1)
-    cross(1, (2,), False)
+    cross(1, (2, 3), False)
+    to_first(5)
     to_second(4)
     both(to_last, 3)
-    cross(1, (3,), False)
-    to_core(5)
-    to_first(5)
+    to_second(5)
     to_last(4)
-    to_second(5)
     to_last(5)
 
     rows = rows_of(r, share)
     for h in range(2):
         total = sums[h, rows, :]
-        for d in (1, 3, 2):
-            arrived(last_in.at[d, h], l_s.at[2 + h], l_r.at[d, h])
-            total = total + last_in[d, h]
+        for core, d in ((k, 1), (1 - k, 1), (k, 3), (1 - k, 3), (k, 2), (1 - k, 2)):
+            arrived(last_in.at[core, d, h], l_s.at[0, 0], l_r.at[core, d, h])
+            total = total + last_in[core, d, h]
         out_ref[:, h * lane:(h + 1) * lane] = total
 
     for copy in pending:
@@ -467,20 +465,20 @@
             pltpu.VMEM((SIDE * pad, columns), BF16),
             pltpu.VMEM((SIDE * pad, columns), BF16),
             pltpu.VMEM((2 * SIDE, window, lane), F32),
-            pltpu.VMEM((2 * SIDE, SIDE, share, lane), F32),
-            pltpu.VMEM((2 * SIDE, 2, share, lane), F32),
-            pltpu.VMEM((2 * SIDE, share, lane), F32),
-            pltpu.VMEM((SIDE, 2, share, lane), F32),
+            pltpu.VMEM((2, SIDE, share, lane), F32),
+            pltpu.VMEM((2 * SIDE, 2, 2 * share, lane), F32),
+            pltpu.VMEM((2 * SIDE, 2 * share, lane), F32),
+            pltpu.VMEM((2, SIDE, 2, share, lane), F32),
             dma((7,)),
             dma((SIDE,)), dma((SIDE,)), dma((3, SIDE)), dma((3, SIDE)),
             dma, dma, dma((2,)), dma((2,)), dma((SIDE,)), dma((SIDE,)),
             dma((3, PARTS)), dma((SIDE, PARTS)),
             dma((SIDE, SIDE)), dma((SIDE, SIDE)),
             dma((2, SIDE)), dma((2, SIDE)), dma((2, SIDE)), dma((2, SIDE)),
-            dma((2 * SIDE, SIDE)), dma((2 * SIDE, SIDE)),
+            dma((2, SIDE)), dma((2, SIDE)),
             dma((2 * SIDE, 2)), dma((2 * SIDE, 2)),
             dma((2 * SIDE,)), dma((2 * SIDE,)),
-            dma((2 * SIDE,)), dma((SIDE, 2)),
+            dma((2, 2 * SIDE)), dma((2, SIDE, 2)),
         ],
         compiler_params=pltpu.CompilerParams(
             collective_id=0, has_side_effects=True, vmem_limit_bytes=65000 * 1024

time: 121 us -> 116 us (0.959)
  Pallas kernels: 119 us -> 114 us
    pallas_call x1, Pallas kernels: 119 us -> 114 us  [per_device(): pl.pallas_call(kernel, out_shape=jax.ShapeDtypeStruct((share, columns), F...]
where the time goes in v2:
time: 116 us
  Pallas kernels  114 us (98%)
  local copies, waits for them, and re-layouts  1.57 us (1%)
    pallas_call x1, Pallas kernels, per_device(): pl.pallas_call(kernel, out_shape=jax.ShapeDtypeStruct((share, columns), F...  114 us

profile of v2, /device:TPU:1, one launch (start us, length us, event | category | flops | bytes accessed | tf_op | source)
XLA Modules:
  0.0 115.5 jit_solution(17251623626153872879)
XLA Ops:
  0.0 114.0 %shard_map.46 = f32[128,256]{1,0:T(8,128)} custom-call(f32[8064,256]{1,0:T(8,128)} %tail_hbm.1, f32[504,1024]{1,0:T(8,128)} %panel_hbm.1, f32[8,1024]{1,0:T(8,128)} %block_hbm.1, f32[128,256]{1,0:T(8,128)} %rhs_hbm.1), custom_call_target="tpu_custom_call" | custom-call | tf_op jit(solution)/shard_map/pallas_call | solution.py:446
  114.0 1.6 %copy.6 = f32[128,256]{1,0:T(8,128)} copy(f32[128,256]{1,0:T(8,128)} %shard_map.46) | data formatting | bytes 262144

commit v3 on v2

--- a/solution.py
+++ b/solution.py
@@ -13,7 +13,7 @@
 BF16 = jnp.bfloat16
 SIDE = 4
 PLACE = (0, 1, 3, 2)
-CUTS = (9, 6, 8, 8, 8, 12, 12)
+CUTS = (13, 8, 7, 5, 10, 10, 10)
 PARTS = len(CUTS)
 FORTH = 4
 
@@ -33,6 +33,12 @@
 def halves(a):
     high = a.astype(BF16)
     return high, (a - high.astype(F32)).astype(BF16)
+
+
+def dot_split(a, b):
+    a_hi, a_lo = halves(a)
+    b_hi, b_lo = halves(b)
+    return mm(a_hi, b_hi) + mm(a_hi, b_lo) + mm(a_lo, b_hi)
 
 
 def lower_inverse(block, base=32):
@@ -175,13 +181,13 @@
 
     def swap_thin(sem, mine, where):
         for d in range(SIDE):
-            thin_copies.append(
-                go(thin_rows(d, mine), thin_rows(d, mine), wy_s.at[sem, d], wy_r.at[sem, d], at_p(where), False)
-            )
+            side = 1 if d < 2 else -1
+            rows = thin_rows(d, side * mine)
+            thin_copies.append(go(rows, rows, wy_s.at[sem, d], wy_r.at[sem, d], at_p(side * where), False))
 
     def thin_here(sem, theirs):
         for d in range(SIDE):
-            arrived(thin_rows(d, theirs), wy_s.at[sem, d], wy_r.at[sem, d])
+            arrived(thin_rows(d, theirs if d < 2 else -theirs), wy_s.at[sem, d], wy_r.at[sem, d])
 
     swap_thin(0, 0, near)
     send_panel(1)
@@ -211,13 +217,12 @@
     go(wall.at[r], wall.at[r], wa_s, wa_r, at_x(p2))
     go(wall.at[r], wall.at[r], wb_s.at[0], wb_r.at[0], at_x(p1))
     strip_to_core(0, x)
-    for i in range(FORTH):
+    for i in range(PARTS - 1):
         pass_panel(i)
     arrived(wall.at[2 * p2 + k], wa_s, wa_r)
     go(wall.at[2 * p2 + k], wall.at[2 * p2 + k], wb_s.at[1], wb_r.at[1], at_x(p1))
     strip_to_core(1, p2)
-    for i in range(FORTH, PARTS):
-        pass_panel(i)
+    pass_panel(PARTS - 1)
 
     for q in (0, 1, 3, 2):
         for d in (1, 3):
@@ -250,8 +255,9 @@
                 start = pl.multiple_of(i * strip, strip)
                 left = inv[pl.ds(base + size + start, strip), low_rows]
                 under = wall[pl.ds(base // share + count, count), :, top].reshape(size, size)
-                tmp[pl.ds(0, strip), pl.ds(0, size)] = dot(left, under)
-                inv[pl.ds(base + size + start, strip), top] = -dot(tmp[pl.ds(0, strip), pl.ds(0, size)], inv[top, top])
+                times = dot if size == share else dot_split
+                tmp[pl.ds(0, strip), pl.ds(0, size)] = times(left, under)
+                inv[pl.ds(base + size + start, strip), top] = -times(tmp[pl.ds(0, strip), pl.ds(0, size)], inv[top, top])
                 return 0
 
             if strip == size:
@@ -396,12 +402,11 @@
     turn_panel(3, 0)
     product(0, (3,), whole, False)
     both(to_core, 0)
-    beside(1, (0, 1), True)
+    beside(1, (0,), True)
     both(to_first, 0)
-    beside(3, (0, 1), True)
-    beside(1, (2, 3), False)
+    beside(1, (1, 2, 3), False)
     both(to_first, 1)
-    beside(3, (2, 3), False)
+    beside(3, (0, 1, 2, 3), True)
     both(to_first, 3)
     both(to_second, 0)
     pass_tail(0)
@@ -411,9 +416,9 @@
     cross(0, (0, 1), True)
     cross(0, (2, 3), False)
     to_first(4)
+    both(to_second, 3)
     both(to_last, 1)
     cross(1, (0, 1), True)
-    both(to_second, 3)
     cross(1, (2, 3), False)
     to_first(5)
     to_second(4)
@@ -445,7 +450,7 @@
     anywhere = pl.BlockSpec(memory_space=pl.ANY)
     return pl.pallas_call(
         kernel,
-        out_shape=jax.ShapeDtypeStruct((share, columns), F32),
+        out_shape=pltpu.VMEM((share, columns), F32),
         in_specs=[anywhere] * 4,
         out_specs=pl.BlockSpec(memory_space=pltpu.VMEM),
         scratch_shapes=[

time: 116 us -> 111 us (0.957)
  Pallas kernels: 114 us -> 110 us
    pallas_call x1, Pallas kernels: 114 us -> 110 us  [per_device(): pl.pallas_call(kernel, out_shape=pltpu.VMEM((share, columns), F32), in_sp...]
where the time goes in v3:
time: 111 us
  Pallas kernels  110 us (99%)
    pallas_call x1, Pallas kernels, per_device(): pl.pallas_call(kernel, out_shape=pltpu.VMEM((share, columns), F32), in_sp...  110 us

profile of v3, /device:TPU:1, one launch (start us, length us, event | category | flops | bytes accessed | tf_op | source)
XLA Modules:
  0.0 110.9 jit_solution(1292155694405372750)
XLA Ops:
  0.0 110.2 %shard_map.46 = f32[128,256]{1,0:T(8,128)S(1)} custom-call(f32[8064,256]{1,0:T(8,128)} %tail_hbm.1, f32[504,1024]{1,0:T(8,128)} %panel_hbm.1, f32[8,1024]{1,0:T(8,128)} %block_hbm.1, f32[128,256]{1,0:T(8,128)} %rhs_hbm.1), custom_call_target="tpu_custom_call" | custom-call | tf_op jit(solution)/shard_map/pallas_call | solution.py:451
  110.2 0.7 copy.6

commit v4 on v3

--- a/solution.py
+++ b/solution.py
@@ -287,7 +287,8 @@
             plo[rows_of(i), :] = rest
             return 0
 
-        lax.fori_loop(0, pad // 128, split_rows, 0)
+        for i in range(pad // 128):
+            split_rows(i, 0)
         place = pl.ds(pl.multiple_of(q * pad, pad), pad)
         for n in range(0, window, 256):
             deep, cols = pl.ds(n, window - n), pl.ds(n, 256)
@@ -309,7 +310,8 @@
     locals_[1].wait()
     panel_here(1)
     panel_here(2)
-    lax.fori_loop(0, 3, turn_panel, 0)
+    for q in range(3):
+        turn_panel(q, 0)
 
     def take_tail(j, places, cols):
         for q in places:
@@ -336,7 +338,8 @@
                 sums[u, rows, :] = piece if fresh else sums[u, rows, :] + piece
             return 0
 
-        lax.fori_loop(0, window // strip, one, 0)
+        for i in range(window // strip):
+            one(i, 0)
 
     whole = pl.ds(0, width)
     def beside(j, places, fresh):

time: 111 us -> 110 us (level)
  no operation moved by 1% of the time
where the time goes in v4:
time: 110 us
  Pallas kernels  109 us (99%)
    pallas_call x1, Pallas kernels, per_device(): pl.pallas_call(kernel, out_shape=pltpu.VMEM((share, columns), F32), in_sp...  109 us

profile of v4, /device:TPU:1, one launch (start us, length us, event | category | flops | bytes accessed | tf_op | source)
XLA Modules:
  0.0 109.9 jit_solution(11998970096112303661)
XLA Ops:
  0.0 109.2 %shard_map.46 = f32[128,256]{1,0:T(8,128)S(1)} custom-call(f32[8064,256]{1,0:T(8,128)} %tail_hbm.1, f32[504,1024]{1,0:T(8,128)} %panel_hbm.1, f32[8,1024]{1,0:T(8,128)} %block_hbm.1, f32[128,256]{1,0:T(8,128)} %rhs_hbm.1), custom_call_target="tpu_custom_call" | custom-call | tf_op jit(solution)/shard_map/pallas_call | solution.py:454
  109.2 0.7 copy.6

commit v5 on v4

--- a/solution.py
+++ b/solution.py
@@ -252,7 +252,7 @@
             top, low_rows = pl.ds(base, size), pl.ds(base + size, size)
 
             def below(i, _, base=base, size=size, count=count, strip=strip, top=top, low_rows=low_rows):
-                start = pl.multiple_of(i * strip, strip)
+                start = i * strip
                 left = inv[pl.ds(base + size + start, strip), low_rows]
                 under = wall[pl.ds(base // share + count, count), :, top].reshape(size, size)
                 times = dot if size == share else dot_split
@@ -260,10 +260,8 @@
                 inv[pl.ds(base + size + start, strip), top] = -times(tmp[pl.ds(0, strip), pl.ds(0, size)], inv[top, top])
                 return 0
 
-            if strip == size:
-                below(0, 0)
-            else:
-                lax.fori_loop(0, size // strip, below, 0)
+            for i in range(size // strip):
+                below(i, 0)
         size *= 2
 
     def split_inverse(i, _):
@@ -272,7 +270,8 @@
         inv_lo[rows_of(i), :] = rest
         return 0
 
-    lax.fori_loop(0, window // 128, split_inverse, 0)
+    for i in range(window // 128):
+        split_inverse(i, 0)
 
     def pass_tail(h):
         for q in range(SIDE):
@@ -352,11 +351,14 @@
             arrived(tbuf.at[2, q, pl.ds(0, depth), pl.ds(h * lane, lane)], f_s.at[h, q], f_r.at[h, q])
         product(2, places, pl.ds(h * lane, lane), fresh)
 
-    def lines(u, xx):
-        return rows_of(xx, 2 * share) if u > 1 else rows_of(2 * xx + k, share)
-
-    def height(u):
-        return pl.ds(0, 2 * share if u > 1 else share)
+    def cores(u):
+        return range(2 if u > 1 else 1)
+
+    def line(u, xx, e):
+        return rows_of(2 * xx + (e if u > 1 else k), share)
+
+    def piece(e):
+        return pl.ds(e * share, share)
 
     def to_core(u):
         for i in range(SIDE):
@@ -369,25 +371,28 @@
                 rows = rows_of(2 * i + k, share)
                 sums[u, rows, :] = sums[u, rows, :] + core_in[u, i]
         for i, other in ((1, p12), (0, p1)):
-            go(sums.at[u, lines(u, other)], first_in.at[u, i, height(u)], a_s.at[u, i], a_r.at[u, i], at_x(p1))
+            for e in cores(u):
+                go(sums.at[u, line(u, other, e)], first_in.at[u, i, piece(e)],
+                   a_s.at[u, i, e], a_r.at[u, i, e], at_x(p1))
 
     def to_second(u):
         for i, other in ((1, p2), (0, x)):
-            arrived(first_in.at[u, i, height(u)], a_s.at[u, i], a_r.at[u, i])
-            rows = lines(u, other)
-            sums[u, rows, :] = sums[u, rows, :] + first_in[u, i, height(u), :]
-            if i == 1:
-                go(sums.at[u, rows], second_in.at[u, height(u)], b_s.at[u], b_r.at[u], at_x(p2))
+            for e in cores(u):
+                arrived(first_in.at[u, i, piece(e)], a_s.at[u, i, e], a_r.at[u, i, e])
+                rows = line(u, other, e)
+                sums[u, rows, :] = sums[u, rows, :] + first_in[u, i, piece(e), :]
+                if i == 1:
+                    go(sums.at[u, rows], second_in.at[u, piece(e)], b_s.at[u, e], b_r.at[u, e], at_x(p2))
 
     def to_last(u):
         j, h = u // 2, u % 2
-        arrived(second_in.at[u, height(u)], b_s.at[u], b_r.at[u])
-        rows = lines(u, x)
-        sums[u, rows, :] = sums[u, rows, :] + second_in[u, height(u), :]
-        if j:
-            for i, core in enumerate((k, 1 - k)):
-                go(sums.at[u, rows_of(2 * x + core, share)], last_in.at[k, SIDE - j, h],
-                   l_s.at[i, u], l_r.at[k, SIDE - j, h], {"row": 2 * x + core, "col": place_at(j, 0)})
+        for e in cores(u):
+            arrived(second_in.at[u, piece(e)], b_s.at[u, e], b_r.at[u, e])
+            rows = line(u, x, e)
+            sums[u, rows, :] = sums[u, rows, :] + second_in[u, piece(e), :]
+            if j:
+                go(sums.at[u, rows], last_in.at[k, SIDE - j, h], l_s.at[e, u], l_r.at[k, SIDE - j, h],
+                   {"row": 2 * x + e, "col": place_at(j, 0)})
 
     def both(stage, j):
         stage(2 * j)
@@ -484,8 +489,8 @@
             dma((SIDE, SIDE)), dma((SIDE, SIDE)),
             dma((2, SIDE)), dma((2, SIDE)), dma((2, SIDE)), dma((2, SIDE)),
             dma((2, SIDE)), dma((2, SIDE)),
+            dma((2 * SIDE, 2, 2)), dma((2 * SIDE, 2, 2)),
             dma((2 * SIDE, 2)), dma((2 * SIDE, 2)),
-            dma((2 * SIDE,)), dma((2 * SIDE,)),
             dma((2, 2 * SIDE)), dma((2, SIDE, 2)),
         ],
         compiler_params=pltpu.CompilerParams(

time: 110 us -> 109 us (level)
    pallas_call x1, Pallas kernels: 109 us -> 108 us  [per_device(): pl.pallas_call(kernel, out_shape=pltpu.VMEM((share, columns), F32), in_sp...]
where the time goes in v5:
time: 109 us
  Pallas kernels  108 us (99%)
    pallas_call x1, Pallas kernels, per_device(): pl.pallas_call(kernel, out_shape=pltpu.VMEM((share, columns), F32), in_sp...  108 us

profile of v5, /device:TPU:1, one launch (start us, length us, event | category | flops | bytes accessed | tf_op | source)
XLA Modules:
  0.0 108.7 jit_solution(9928353676432237899)
XLA Ops:
  0.0 108.0 %shard_map.46 = f32[128,256]{1,0:T(8,128)S(1)} custom-call(f32[8064,256]{1,0:T(8,128)} %tail_hbm.1, f32[504,1024]{1,0:T(8,128)} %panel_hbm.1, f32[8,1024]{1,0:T(8,128)} %block_hbm.1, f32[128,256]{1,0:T(8,128)} %rhs_hbm.1), custom_call_target="tpu_custom_call" | custom-call | tf_op jit(solution)/shard_map/pallas_call | solution.py:459
  108.0 0.7 copy.6

commit v6 on v5

--- a/solution.py
+++ b/solution.py
@@ -429,11 +429,11 @@
     cross(1, (0, 1), True)
     cross(1, (2, 3), False)
     to_first(5)
-    to_second(4)
     both(to_last, 3)
     to_second(5)
+    to_second(4)
+    to_last(5)
     to_last(4)
-    to_last(5)
 
     rows = rows_of(r, share)
     for h in range(2):

time: 109 us -> 110 us (level)
    pallas_call x1, Pallas kernels: 108 us -> 109 us  [per_device(): pl.pallas_call(kernel, out_shape=pltpu.VMEM((share, columns), F32), in_sp...]
where the time goes in v6:
time: 110 us
  Pallas kernels  109 us (99%)
    pallas_call x1, Pallas kernels, per_device(): pl.pallas_call(kernel, out_shape=pltpu.VMEM((share, columns), F32), in_sp...  109 us

profile of v6, /device:TPU:1, one launch (start us, length us, event | category | flops | bytes accessed | tf_op | source)
XLA Modules:
  0.0 110.0 jit_solution(1426426421182484656)
XLA Ops:
  0.0 109.4 %shard_map.46 = f32[128,256]{1,0:T(8,128)S(1)} custom-call(f32[8064,256]{1,0:T(8,128)} %tail_hbm.1, f32[504,1024]{1,0:T(8,128)} %panel_hbm.1, f32[8,1024]{1,0:T(8,128)} %block_hbm.1, f32[128,256]{1,0:T(8,128)} %rhs_hbm.1), custom_call_target="tpu_custom_call" | custom-call | tf_op jit(solution)/shard_map/pallas_call | solution.py:459
  109.4 0.7 copy.6
